TPU v7x, 128 devices: a whole 4x4x4 slice. The times are simulated.
128 devices in a mesh: grp: 4 (over z), tile: 32 (over x, y, core).
Axes of the slice: x: 4, y: 4, z: 4, core: 2. Of those that a mesh axis runs over, the one named last changes fastest.
Arguments:
- noise: bfloat16 [16, 3, 2048, 2048], P('grp', None, 'tile'), may hold values from -6 to 6
- stress: float32 [6, 2048, 2048], P(None, 'tile', 'grp'), as said below
- timescale: float32 [2048, 2048], P('tile', 'grp'), may hold values from 3 to 256
- mean_inflow: float32 [2048, 2048], P('tile', 'grp'), may hold values from 0.5 to 1.5
- courant: float32 [2048, 2048], P('tile', 'grp'), may hold values from 0.2 to 0.9
- prior_state: float32 [3, 2048, 2048], P(None, 'tile', 'grp'), may hold values from -6 to 6
- field: float32 [3, 8, 2048, 2048], P(None, None, 'tile', 'grp'), may hold values from -6 to 6
Outputs:
- inflow: bfloat16 [16, 3, 2048, 2048], P(None, None, 'tile', 'grp')
- field_out: float32 [3, 8, 2048, 2048], P(None, None, 'tile', 'grp')
Inputs may be any that keep to these rules, and one draw needn't show every extreme that they name: stress holds, per cell, R11, R21, R22, R31, R32, R33 of a symmetric positive definite tensor whose Cholesky factor has diagonal entries of 0.3 or more.
All inputs are finite; a program needn't handle non-finite values.
Results may differ from a plain program's by a relative error of at most 0.0085.
Values may be sent and summed in bfloat16 or wider, within the bound.
A program may use at most 128 MiB of HBM per device.

v0:
```python
import math
import jax
import jax.numpy as jnp
from jax import lax
from jax.sharding import PartitionSpec as P

LS = 2
FW = 4


def padded_2(value, sides, width, wrap):
    for axis, dim in sides:
        devices, length = (lax.axis_size(axis), value.shape[dim])
        up = [(i, (i + 1) % devices) for i in range(devices if wrap else devices - 1)]
        down = [(j, i) for i, j in up]
        last = lax.slice_in_dim(value, length - width, length, axis=dim)
        initial = lax.slice_in_dim(value, 0, width, axis=dim)
        before = lax.ppermute(last, axis, up)
        after = lax.ppermute(initial, axis, down)
        value = jnp.concatenate([before, value, after], axis=dim)
    return value


def filter_taps():
    offsets = jnp.arange(-FW, FW + 1).astype(jnp.float32)
    raw = jnp.exp(-math.pi * offsets * offsets / (2.0 * LS * LS))
    return (raw / jnp.sqrt(jnp.sum(raw * raw))).astype(jnp.bfloat16)


def band_matrix(rows, taps):
    width = taps.shape[0]
    distance = jnp.arange(rows + width - 1)[None, :] - jnp.arange(rows)[:, None]
    picks = distance[:, :, None] == jnp.arange(width)[None, None, :]
    return jnp.sum(jnp.where(picks, taps.astype(jnp.float32), 0.0), axis=2).astype(jnp.bfloat16)


def filter_last(padded, taps):
    width = taps.shape[0]
    length = padded.shape[-1] - width + 1
    block = math.gcd(length, 128)
    weights = band_matrix(block, taps)
    windows = jnp.stack(
        [
            lax.slice_in_dim(padded, start, start + block + width - 1, axis=padded.ndim - 1)
            for start in range(0, length, block)
        ],
        axis=-2,
    )
    result = jnp.einsum("...kw,bw->...kb", windows, weights, preferred_element_type=jnp.float32)
    return result.reshape(result.shape[:-2] + (length,))


def filter_rows(padded, taps):
    rows = padded.shape[2] - taps.shape[0] + 1
    weights = band_matrix(rows, taps)
    return jnp.einsum("ij,pcjz->pciz", weights, padded, preferred_element_type=jnp.float32)


def cholesky_cells(stress):
    first_diag = jnp.sqrt(stress[0])
    second_low = stress[1] / first_diag
    second_diag = jnp.sqrt(stress[2] - second_low * second_low)
    third_low = stress[3] / first_diag
    third_mid = (stress[4] - second_low * third_low) / second_diag
    third_diag = jnp.sqrt(stress[5] - third_low * third_low - third_mid * third_mid)
    return (first_diag, second_low, second_diag, third_low, third_mid, third_diag)


def velocity_of(state, factors, mean_inflow):
    first_diag, second_low, second_diag, third_low, third_mid, third_diag = factors
    return jnp.stack(
        [
            mean_inflow + first_diag * state[0],
            second_low * state[0] + second_diag * state[1],
            third_low * state[0] + third_mid * state[1] + third_diag * state[2],
        ]
    )


def march(current, courant, velocity):
    upstream = jnp.concatenate([velocity[:, None], current[:, :-1]], axis=1)
    return (1.0 - courant) * current + courant * upstream


def tile_chain(filtered, stress, timescale, mean_inflow, courant, prior_state, field):
    decay = jnp.exp(-math.pi / (2.0 * timescale))
    gain = jnp.sqrt(1.0 - decay * decay)
    factors = cholesky_cells(stress)

    def advance(carry, plane):
        state, current = carry
        state = decay * state + gain * plane
        velocity = velocity_of(state, factors, mean_inflow)
        return ((state, march(current, courant, velocity)), velocity.astype(jnp.bfloat16))

    (state, result), inflow = lax.scan(advance, (prior_state, field), filtered)
    return (inflow, result)


def body(noise, stress, timescale, mean_inflow, courant, prior_state, field):
    taps = filter_taps()
    flipped = jnp.swapaxes(noise, 2, 3)
    tiles = lax.all_to_all(
        lax.all_to_all(flipped, "tile", split_axis=2, concat_axis=3, tiled=True),
        "grp",
        split_axis=3,
        concat_axis=0,
        tiled=True,
    )
    banded = padded_2(tiles, (("grp", 3),), FW, False)
    widened = padded_2(banded, (("tile", 2),), FW, True)
    span = filter_rows(widened, taps).astype(jnp.bfloat16)
    filtered = filter_last(span, taps)
    inflow, result = tile_chain(
        filtered, stress, timescale, mean_inflow, courant, prior_state, field
    )
    return (inflow, result)


def solution(mesh):
    placed = (
        P("grp", None, "tile", None),
        P(None, "tile", "grp"),
        P("tile", "grp"),
        P("tile", "grp"),
        P("tile", "grp"),
        P(None, "tile", "grp"),
        P(None, None, "tile", "grp"),
    )
    return jax.shard_map(
        body,
        mesh=mesh,
        in_specs=placed,
        out_specs=(P(None, None, "tile", "grp"), P(None, None, "tile", "grp")),
        check_vma=False,
    )
```

profile of v0, /device:TPU:63, one launch (start us, length us, event | category | flops | bytes accessed | tf_op | source)
XLA Modules:
  0.0 310.5 jit_solution(12647594609920412347)
XLA Ops:
  0.6 1.9 copy-done.7
  2.5 7.1 %copy.41 = bf16[4,3,64,2048]{2,0,1,3:T(4,128)(2,1)} copy(bf16[4,3,64,2048]{3,2,1,0:T(8,128)(2,1)S(1)} %copy-done.7) | data formatting | bytes 6291456 | tf_op args[0]
  9.6 7.7 %bitcast_bitcast_fusion = bf16[2048,3,4,64]{3,2,1,0:T(4,128)(2,1)} fusion(bf16[4,3,64,2048]{2,0,1,3:T(4,128)(2,1)} %copy.41), kind=kLoop, calls=%fused_computation.73 | loop fusion | bytes 6291456
  17.3 7.5 %reshape.107 = bf16[32,2,24576]{2,1,0:T(2,128)(2,1)S(1)} reshape(bf16[2048,3,4,64]{3,2,1,0:T(4,128)(2,1)} %bitcast_bitcast_fusion) | data formatting | bytes 6291456
  24.8 43.9 %all_to_all.36 = bf16[32,2,24576]{2,1,0:T(2,128)(2,1)} all-to-all(bf16[32,2,24576]{2,1,0:T(2,128)(2,1)S(1)} %reshape.107), channel_id=1, replica_groups=mesh['grp'=4,'tile'=32] {'tile'}, dimensions={0} | all-to-all | bytes 6291456 | tf_op jit(solution)/shard_map/all_to_all | solution.py:104
  68.7 8.7 %reshape.108 = bf16[2048,3,4,64]{3,2,1,0:T(4,128)(2,1)} reshape(bf16[32,2,24576]{2,1,0:T(2,128)(2,1)} %all_to_all.36) | data formatting | bytes 6291456
  77.4 9.5 %copy.65 = bf16[4,3,32,64,64]{4,2,3,1,0:T(8,128)(2,1)} copy(bf16[4,3,32,64,64]{4,0,1,3,2:T(4,128)(2,1)} %bitcast.127) | data formatting | bytes 6291456 | tf_op jit(solution)/shard_map/all_to_all | solution.py:104
  86.9 11.8 %copy.54 = bf16[4,3,64,32,64]{2,0,1,4,3:T(4,128)(2,1)} copy(bf16[4,3,64,32,64]{4,3,2,1,0:T(8,128)(2,1)} %bitcast.128) | data formatting | bytes 6291456 | tf_op jit(solution)/shard_map/all_to_all | solution.py:104
  98.7 7.7 %reshape.109 = bf16[4,2,196608]{2,1,0:T(2,128)(2,1)} reshape(bf16[2048,3,4,64]{3,2,1,0:T(4,128)(2,1)} %bitcast.129) | data formatting | bytes 6291456
  106.5 5.0 %all-to-all-start.1 = ((bf16[4,2,196608]{2,1,0:T(2,128)(2,1)}), bf16[4,2,196608]{2,1,0:T(2,128)(2,1)S(1)}, u32[]{:S(2)}, u32[]{:S(2)}) async-start(bf16[4,2,196608]{2,1,0:T(2,128)(2,1)} %reshape.109), calls=%async_computation.1 | async-start | bytes 6291456 | tf_op jit(solution)/shard_map/all_to_all | solution.py:103
  112.9 2.2 fusion.24
  115.8 1.6 fusion.26
  117.4 30.1 %all-to-all-done.1 = bf16[4,2,196608]{2,1,0:T(2,128)(2,1)S(1)} async-done(((bf16[4,2,196608]{2,1,0:T(2,128)(2,1)}), bf16[4,2,196608]{2,1,0:T(2,128)(2,1)S(1)}, u32[]{:S(2)}, u32[]{:S(2)}) %all-to-all-start.1) | async-done | bytes 3145760 | tf_op jit(solution)/shard_map/all_to_all | solution.py:103
  147.5 5.3 %reshape.110 = bf16[2048,3,4,64]{3,2,1,0:T(4,128)(2,1)} reshape(bf16[4,2,196608]{2,1,0:T(2,128)(2,1)S(1)} %all-to-all-done.1) | data formatting | bytes 6291456
  152.8 8.3 %copy.45 = bf16[4,4,3,64,512]{4,3,2,1,0:T(8,128)(2,1)S(1)} copy(bf16[4,4,3,64,512]{3,1,2,4,0:T(4,128)(2,1)} %bitcast.130) | data formatting | bytes 6291456 | tf_op jit(solution)/shard_map/all_to_all | solution.py:103
  161.1 1.5 fusion.38
  162.6 1.5 copy.46
  164.1 1.5 copy.47
  165.7 3.1 collective-permute-start.1
  168.8 2.4 collective-permute-start
  171.3 2.3 collective-permute-done
  176.1 1.8 pad_maximum_fusion.3
  177.9 5.7 %collective-permute-start.2 = (bf16[16,3,4,520]{3,2,1,0:T(4,128)(2,1)S(1)}, bf16[16,3,4,520]{3,2,1,0:T(4,128)(2,1)S(1)}, u32[]{:S(2)}, u32[]{:S(2)}) collective-permute-start(bf16[16,3,4,520]{3,2,1,0:T(4,128)(2,1)S(1)} %get-tuple-element.126), channel_id=1, source_target_pairs={{0,1},{1,2},{2,3},{3,4},{4,5},{5,6},{6,7},{7,8},{8,9},{9,10},{10,1... | collective-permute-start | bytes 599048 | tf_op jit(solution)/shard_map/ppermute | solution.py:18
  183.6 1.6 sqrt_bitcast_fusion
  185.2 1.5 collective-permute-done.2
  186.7 5.8 %collective-permute-done.3 = bf16[16,3,4,520]{3,2,1,0:T(4,128)(2,1)S(1)} collective-permute-done((bf16[16,3,4,520]{3,2,1,0:T(4,128)(2,1)S(1)}, bf16[16,3,4,520]{3,2,1,0:T(4,128)(2,1)S(1)}, u32[]{:S(2)}, u32[]{:S(2)}) %collective-permute-start.3) | collective-permute-done | bytes 199712 | tf_op jit(solution)/shard_map/ppermute | solution.py:19
  192.5 4.2 %convert_bitcast_fusion.3 = bf16[16,3,64,520]{3,2,1,0:T(8,128)(2,1)S(1)} fusion(bf16[16,3,4,520]{3,2,1,0:T(4,128)(2,1)S(1)} %collective-permute-done.3, bf16[16,3,64,4]{3,2,1,0:T(8,128)(2,1)S(1)} %copy-done.6, bf16[16,3,64,512]{3,2,1,0:T(8,128)(2,1)S(1)} %bitcast.133, bf16[16,3,64,4]{3,2,1,0:T(8,128)(2,1)S(1)} %copy-done.5, ...), kind=kOutput, calls=%fused_computation.35 | convolution fusion | flops 249600000 | bytes 6798336 | tf_op jit(solution)/shard_map/ij,pcjz->pciz/dot_general | solution.py:56
  197.6 2.6 fusion.18
  200.2 3.5 %copy.64 = f32[16,3,4,8,8,128]{5,4,2,3,1,0:T(8,128)} copy(f32[16,3,4,8,8,128]{5,4,3,2,1,0:T(8,128)S(1)} %fusion.18) | data formatting | bytes 12582912 | tf_op jit(solution)/shard_map/reshape | solution.py:50
  203.7 105.1 %while.14 = (s32[]{:T(128)}, f32[3,64,512]{2,1,0:T(8,128)S(1)}, f32[3,8,64,512]{3,2,1,0:T(8,128)S(1)}, bf16[16,3,64,512]{3,2,1,0:T(8,128)(2,1)}, f32[64,512]{1,0...) while((s32[]{:T(128)}, f32[3,64,512]{2,1,0:T(8,128)S(1)}, ...), condition=%wide.region_4.5_spmd, body=%wide.region_3.4_spmd.sunk | while | flops 4685826 | bytes 20512960 | solution.py:96
  205.9 1.4 convert_bitcast_fusion.5
  208.2 1.4 fusion.42
  212.5 1.4 convert_bitcast_fusion.5
  219.0 1.4 convert_bitcast_fusion.5
  225.6 1.4 convert_bitcast_fusion.5
  232.2 1.4 convert_bitcast_fusion.5
  238.7 1.4 convert_bitcast_fusion.5
  245.3 1.4 convert_bitcast_fusion.5
  251.9 1.4 convert_bitcast_fusion.5
  258.4 1.4 convert_bitcast_fusion.5
  265.0 1.4 convert_bitcast_fusion.5
  271.6 1.4 convert_bitcast_fusion.5
  278.2 1.4 convert_bitcast_fusion.5
  284.7 1.4 convert_bitcast_fusion.5
  291.3 1.4 convert_bitcast_fusion.5
  297.9 1.4 convert_bitcast_fusion.5
  304.4 1.4 convert_bitcast_fusion.5
  308.8 1.7 copy-done
  (153 shorter events, 86.1 us)
Async XLA Ops:
  0.6 1.9 copy-start.7
  106.5 6.5 %copy-start.8 = (f32[64,512]{1,0:T(8,128)S(1)}, f32[64,512]{1,0:T(8,128)}, u32[]{:S(2)}) copy-start(f32[64,512]{1,0:T(8,128)} %param.11) | copy-start | bytes 393220
  106.5 41.0 %all-to-all-start.1 = ((bf16[4,2,196608]{2,1,0:T(2,128)(2,1)}), bf16[4,2,196608]{2,1,0:T(2,128)(2,1)S(1)}, u32[]{:S(2)}, u32[]{:S(2)}) async-start(bf16[4,2,196608]{2,1,0:T(2,128)(2,1)} %reshape.109), calls=%async_computation.1 | async-start | bytes 6291456 | tf_op jit(solution)/shard_map/all_to_all | solution.py:103
  115.1 0.7 copy-start.4
  165.7 9.2 %collective-permute-start.1 = (bf16[16,3,64,4]{2,0,3,1:T(8,128)(2,1)S(1)}, bf16[16,3,64,4]{2,0,3,1:T(8,128)(2,1)S(1)}, u32[]{:S(2)}, u32[]{:S(2)}) collective-permute-start(bf16[16,3,64,4]{2,0,3,1:T(8,128)(2,1)S(1)} %copy.47), channel_id=1, source_target_pairs={{32,0},{64,32},{96,64},{33,1},{65,33},{97,65},{34,2},{66,34},{98,6... | collective-permute-start | bytes 73736 | tf_op jit(solution)/shard_map/ppermute | solution.py:19
  168.8 4.8 %collective-permute-start = (bf16[16,3,64,4]{2,0,3,1:T(8,128)(2,1)S(1)}, bf16[16,3,64,4]{2,0,3,1:T(8,128)(2,1)S(1)}, u32[]{:S(2)}, u32[]{:S(2)}) collective-permute-start(bf16[16,3,64,4]{2,0,3,1:T(8,128)(2,1)S(1)} %copy.46), channel_id=1, source_target_pairs={{0,32},{32,64},{64,96},{1,33},{33,65},{65,97},{2,34},{34,66},{66,9... | collective-permute-start | bytes 73736 | tf_op jit(solution)/shard_map/ppermute | solution.py:18
  176.1 16.4 %copy-start.5 = (bf16[16,3,64,4]{3,2,1,0:T(8,128)(2,1)S(1)}, bf16[16,3,64,4]{3,2,1,0:T(8,128)(2,1)}, u32[]{:S(2)}) copy-start(bf16[16,3,64,4]{3,2,1,0:T(8,128)(2,1)} %copy.48) | copy-start | bytes 73732
  176.1 16.4 %copy-start.6 = (bf16[16,3,64,4]{3,2,1,0:T(8,128)(2,1)S(1)}, bf16[16,3,64,4]{3,2,1,0:T(8,128)(2,1)}, u32[]{:S(2)}) copy-start(bf16[16,3,64,4]{3,2,1,0:T(8,128)(2,1)} %copy.49) | copy-start | bytes 73732
  177.9 8.8 %collective-permute-start.2 = (bf16[16,3,4,520]{3,2,1,0:T(4,128)(2,1)S(1)}, bf16[16,3,4,520]{3,2,1,0:T(4,128)(2,1)S(1)}, u32[]{:S(2)}, u32[]{:S(2)}) collective-permute-start(bf16[16,3,4,520]{3,2,1,0:T(4,128)(2,1)S(1)} %get-tuple-element.126), channel_id=1, source_target_pairs={{0,1},{1,2},{2,3},{3,4},{4,5},{5,6},{6,7},{7,8},{8,9},{9,10},{10,1... | collective-permute-start | bytes 599048 | tf_op jit(solution)/shard_map/ppermute | solution.py:18
  183.6 8.9 %collective-permute-start.3 = (bf16[16,3,4,520]{3,2,1,0:T(4,128)(2,1)S(1)}, bf16[16,3,4,520]{3,2,1,0:T(4,128)(2,1)S(1)}, u32[]{:S(2)}, u32[]{:S(2)}) collective-permute-start(bf16[16,3,4,520]{3,2,1,0:T(4,128)(2,1)S(1)} %get-tuple-element.127), channel_id=1, source_target_pairs={{1,0},{2,1},{3,2},{4,3},{5,4},{6,5},{7,6},{8,7},{9,8},{10,9},{11,1... | collective-permute-start | bytes 599048 | tf_op jit(solution)/shard_map/ppermute | solution.py:19
  200.2 3.5 %copy-start.1 = (f32[3,8,64,512]{3,2,1,0:T(8,128)S(1)}, f32[3,8,64,512]{3,2,1,0:T(8,128)}, u32[]{:S(2)}) copy-start(f32[3,8,64,512]{3,2,1,0:T(8,128)} %param.15) | copy-start | bytes 9437188
  200.2 3.5 %copy-start.2 = (f32[3,64,512]{2,1,0:T(8,128)S(1)}, f32[3,64,512]{2,1,0:T(8,128)}, u32[]{:S(2)}) copy-start(f32[3,64,512]{2,1,0:T(8,128)} %param.14) | copy-start | bytes 1179652
  207.3 0.9 copy-start.3
  213.8 0.9 copy-start.3
  220.4 0.9 copy-start.3
  227.0 0.9 copy-start.3
  233.6 0.9 copy-start.3
  240.1 0.9 copy-start.3
  246.7 0.9 copy-start.3
  253.3 0.9 copy-start.3
  259.8 0.9 copy-start.3
  266.4 0.9 copy-start.3
  273.0 0.9 copy-start.3
  279.5 0.9 copy-start.3
  286.1 0.9 copy-start.3
  292.7 0.9 copy-start.3
  299.3 0.9 copy-start.3
  305.8 0.9 copy-start.3
  308.8 1.7 copy-start
where the time goes:
time: 313 us; the launch traced here: 310 us
  local copies, waits for them, and re-layouts  105 us (34%)
  other arithmetic  97.3 us (31%)
  blocking collectives  43.9 us (14%)
  waiting for transfers between devices  39.8 us (13%)
  starting transfers between devices  16.1 us (5%)
  matrix products  6.73 us (2%)
    unnamed x22, local copies, waits for them, and re-layouts  48.3 us
    all_to_all x1, blocking collectives, body(): lax.all_to_all(flipped, 'tile', split_axis=2, concat_axis=3, tiled=True)  43.9 us
    all_to_all x1, waiting for transfers between devices, body(): lax.all_to_all(lax.all_to_all(flipped, 'tile', split_axis=2, concat_axis=...  30.1 us
    another operation x16, other arithmetic, velocity_of(): jnp.stack([mean_inflow + first_diag * state[0], second_low * state[0] + s...  22.1 us
    add x16, other arithmetic, march(): return (1.0 - courant) * current + courant * upstream  22.1 us
    all_to_all x2, local copies, waits for them, and re-layouts, body(): lax.all_to_all(flipped, 'tile', split_axis=2, concat_axis=3, tiled=True)  21.3 us
    add x16, other arithmetic, advance(): state = decay * state + gain * plane  20.4 us
    sub x16, other arithmetic, march(): return (1.0 - courant) * current + courant * upstream  14.6 us
  transfers between devices with their start and end apart: 5, of which 4 were waited for; matrix products, arithmetic and copies ran while one was open for 2% of the time, Pallas kernels for 0%

commit v1 on v0

--- a/solution.py
+++ b/solution.py
@@ -6,6 +6,13 @@
 
 LS = 2
 FW = 4
+
+
+def trade_parts(x, axis, split, join):
+    peers = lax.axis_size(axis)
+    tiles = jnp.stack(jnp.split(x, peers, axis=split), axis=0)
+    tiles = lax.all_to_all(tiles, axis, split_axis=0, concat_axis=0)
+    return jnp.concatenate(tiles, axis=join)
 
 
 def padded_2(value, sides, width, wrap):
@@ -101,11 +108,7 @@
     taps = filter_taps()
     flipped = jnp.swapaxes(noise, 2, 3)
     tiles = lax.all_to_all(
-        lax.all_to_all(flipped, "tile", split_axis=2, concat_axis=3, tiled=True),
-        "grp",
-        split_axis=3,
-        concat_axis=0,
-        tiled=True,
+        trade_parts(flipped, "tile", 2, 3), "grp", split_axis=3, concat_axis=0, tiled=True
     )
     banded = padded_2(tiles, (("grp", 3),), FW, False)
     widened = padded_2(banded, (("tile", 2),), FW, True)

time: 313 us -> 289 us (0.923)
  local copies, waits for them, and re-layouts: 105 us -> 78.4 us
    all_to_all x3 -> x1, local copies, waits for them, and re-layouts: 29.5 us -> 8.27 us  [body(): lax.all_to_all(trade_parts(flipped, 'tile', 2, 3), 'grp', split_axis=3, c...]
    reshape x0 -> x2, local copies, waits for them, and re-layouts: none -> 12.8 us  [trade_parts(): return jnp.concatenate(tiles, axis=join)]
    while x32, local copies, waits for them, and re-layouts: 9.15 us -> 0.06 us
    unnamed x22 -> x49, local copies, waits for them, and re-layouts: 48.3 us -> 39.6 us
  transfers between devices with their start and end apart: 5 -> 5, of which waited for: 4 -> 4; matrix products, arithmetic and copies ran while one was open for 2% -> 3% of each run, Pallas kernels for 0% -> 0%
where the time goes in v1:
time: 289 us; the launch traced here: 287 us
  other arithmetic  98.4 us (34%)
  local copies, waits for them, and re-layouts  78.4 us (27%)
  blocking collectives  43.9 us (15%)
  waiting for transfers between devices  40 us (14%)
  starting transfers between devices  16 us (6%)
  matrix products  7.9 us (3%)
    all_to_all x1, blocking collectives, trade_parts(): tiles = lax.all_to_all(tiles, axis, split_axis=0, concat_axis=0)  43.9 us
    unnamed x49, local copies, waits for them, and re-layouts  39.6 us
    all_to_all x1, waiting for transfers between devices, body(): lax.all_to_all(trade_parts(flipped, 'tile', 2, 3), 'grp', split_axis=3, c...  30.1 us
    another operation x16, other arithmetic, velocity_of(): jnp.stack([mean_inflow + first_diag * state[0], second_low * state[0] + s...  22.1 us
    add x16, other arithmetic, march(): return (1.0 - courant) * current + courant * upstream  22.1 us
    add x16, other arithmetic, advance(): state = decay * state + gain * plane  20.4 us
    sub x16, other arithmetic, march(): return (1.0 - courant) * current + courant * upstream  15.8 us
    reshape x2, local copies, waits for them, and re-layouts, trade_parts(): return jnp.concatenate(tiles, axis=join)  12.8 us
  transfers between devices with their start and end apart: 5, of which 4 were waited for; matrix products, arithmetic and copies ran while one was open for 3% of the time, Pallas kernels for 0%

profile of v1, /device:TPU:63, one launch (start us, length us, event | category | flops | bytes accessed | tf_op | source)
XLA Modules:
  0.0 286.9 jit_solution(739546389769858706)
XLA Ops:
  0.6 1.9 copy-done.4
  6.3 2.6 copy-done.5
  8.9 7.5 %reshape.115 = bf16[32,2,24576]{2,1,0:T(2,128)(2,1)S(1)} reshape(bf16[32,4,3,64,64]{4,3,2,1,0:T(8,128)(2,1)} %bitcast.290) | data formatting | bytes 6291456
  16.5 43.9 %all_to_all.23 = bf16[32,2,24576]{2,1,0:T(2,128)(2,1)} all-to-all(bf16[32,2,24576]{2,1,0:T(2,128)(2,1)S(1)} %reshape.115), channel_id=1, replica_groups=mesh['grp'=4,'tile'=32] {'tile'}, dimensions={0} | all-to-all | bytes 6291456 | tf_op jit(solution)/shard_map/all_to_all | solution.py:14
  60.4 8.7 %reshape.116 = bf16[32,4,3,64,64]{4,3,2,1,0:T(8,128)(2,1)} reshape(bf16[32,2,24576]{2,1,0:T(2,128)(2,1)} %all_to_all.23) | data formatting | bytes 6291456
  69.1 4.3 %bitcast_bitcast_fusion = bf16[4,3,64,32,64]{2,4,1,0,3:T(8,128)(2,1)S(1)} fusion(bf16[32,4,3,64,64]{4,3,2,1,0:T(8,128)(2,1)} %reshape.116), kind=kLoop, calls=%fused_computation.136 | loop fusion | bytes 6291456 | tf_op jit(solution)/shard_map/reshape | solution.py:15
  73.4 8.5 %copy.51 = bf16[4,3,64,32,64]{2,0,1,4,3:T(4,128)(2,1)} copy(bf16[4,3,64,32,64]{2,4,1,0,3:T(8,128)(2,1)S(1)} %bitcast_bitcast_fusion) | data formatting | bytes 6291456 | tf_op jit(solution)/shard_map/reshape | solution.py:15
  81.9 7.8 %reshape.117 = bf16[4,2,196608]{2,1,0:T(2,128)(2,1)} reshape(bf16[2048,3,4,64]{3,2,1,0:T(4,128)(2,1)} %bitcast.252) | data formatting | bytes 6291456
  89.6 4.9 %all-to-all-start.1 = ((bf16[4,2,196608]{2,1,0:T(2,128)(2,1)}), bf16[4,2,196608]{2,1,0:T(2,128)(2,1)S(1)}, u32[]{:S(2)}, u32[]{:S(2)}) async-start(bf16[4,2,196608]{2,1,0:T(2,128)(2,1)} %reshape.117), calls=%async_computation.1 | async-start | bytes 6291456 | tf_op jit(solution)/shard_map/all_to_all | solution.py:110
  96.0 2.2 fusion.56
  98.8 1.6 fusion.58
  100.4 30.1 %all-to-all-done.1 = bf16[4,2,196608]{2,1,0:T(2,128)(2,1)S(1)} async-done(((bf16[4,2,196608]{2,1,0:T(2,128)(2,1)}), bf16[4,2,196608]{2,1,0:T(2,128)(2,1)S(1)}, u32[]{:S(2)}, u32[]{:S(2)}) %all-to-all-start.1) | async-done | bytes 3145760 | tf_op jit(solution)/shard_map/all_to_all | solution.py:110
  130.6 5.3 %reshape.118 = bf16[2048,3,4,64]{3,2,1,0:T(4,128)(2,1)} reshape(bf16[4,2,196608]{2,1,0:T(2,128)(2,1)S(1)} %all-to-all-done.1) | data formatting | bytes 6291456
  135.8 8.3 %copy.42 = bf16[4,4,3,64,512]{4,3,2,1,0:T(8,128)(2,1)S(1)} copy(bf16[4,4,3,64,512]{3,1,2,4,0:T(4,128)(2,1)} %bitcast.253) | data formatting | bytes 6291456 | tf_op jit(solution)/shard_map/all_to_all | solution.py:110
  144.1 1.5 fusion.70
  145.7 1.5 copy.43
  147.2 1.5 copy.44
  148.7 3.3 %collective-permute-start.1 = (bf16[16,3,64,4]{2,0,3,1:T(8,128)(2,1)S(1)}, bf16[16,3,64,4]{2,0,3,1:T(8,128)(2,1)S(1)}, u32[]{:S(2)}, u32[]{:S(2)}) collective-permute-start(bf16[16,3,64,4]{2,0,3,1:T(8,128)(2,1)S(1)} %copy.44), channel_id=1, source_target_pairs={{32,0},{64,32},{96,64},{33,1},{65,33},{97,65},{34,2},{66,34},{98,6... | collective-permute-start | bytes 73736 | tf_op jit(solution)/shard_map/ppermute | solution.py:26
  152.0 2.2 collective-permute-start
  154.3 2.5 collective-permute-done
  159.4 1.7 pad_maximum_fusion.3
  161.1 5.7 %collective-permute-start.2 = (bf16[16,3,4,520]{3,2,1,0:T(4,128)(2,1)S(1)}, bf16[16,3,4,520]{3,2,1,0:T(4,128)(2,1)S(1)}, u32[]{:S(2)}, u32[]{:S(2)}) collective-permute-start(bf16[16,3,4,520]{3,2,1,0:T(4,128)(2,1)S(1)} %get-tuple-element.126), channel_id=1, source_target_pairs={{0,1},{1,2},{2,3},{3,4},{4,5},{5,6},{6,7},{7,8},{8,9},{9,10},{10,1... | collective-permute-start | bytes 599048 | tf_op jit(solution)/shard_map/ppermute | solution.py:25
  166.7 1.6 sqrt_bitcast_fusion
  168.3 1.6 collective-permute-done.2
  169.9 5.8 %collective-permute-done.3 = bf16[16,3,4,520]{3,2,1,0:T(4,128)(2,1)S(1)} collective-permute-done((bf16[16,3,4,520]{3,2,1,0:T(4,128)(2,1)S(1)}, bf16[16,3,4,520]{3,2,1,0:T(4,128)(2,1)S(1)}, u32[]{:S(2)}, u32[]{:S(2)}) %collective-permute-start.3) | collective-permute-done | bytes 199712 | tf_op jit(solution)/shard_map/ppermute | solution.py:26
  175.7 5.3 %convert_bitcast_fusion.3 = bf16[16,3,64,520]{3,2,1,0:T(8,128)(2,1)S(1)} fusion(bf16[16,3,4,520]{3,2,1,0:T(4,128)(2,1)S(1)} %collective-permute-done.3, bf16[16,3,64,4]{3,2,1,0:T(8,128)(2,1)} %copy.46, bf16[16,3,64,512]{3,2,1,0:T(8,128)(2,1)S(1)} %bitcast.256, bf16[16,3,64,4]{3,2,1,0:T(8,128)(2,1)} %copy.45, ...), kind=kOutput, calls=%fused_computation.34 | convolution fusion | flops 249600000 | bytes 6798336 | tf_op jit(solution)/shard_map/ij,pcjz->pciz/dot_general | solution.py:63
  181.9 2.6 fusion.18
  184.5 3.5 %copy.61 = f32[16,3,4,8,8,128]{5,4,2,3,1,0:T(8,128)} copy(f32[16,3,4,8,8,128]{5,4,3,2,1,0:T(8,128)S(1)} %fusion.18) | data formatting | bytes 12582912 | tf_op jit(solution)/shard_map/reshape | solution.py:57
  188.0 97.2 %while.14 = (s32[]{:T(128)}, f32[3,64,512]{2,1,0:T(8,128)S(1)}, f32[3,8,64,512]{3,2,1,0:T(8,128)S(1)}, bf16[16,3,64,512]{3,2,1,0:T(8,128)(2,1)}, f32[64,512]{1,0...) while((s32[]{:T(128)}, f32[3,64,512]{2,1,0:T(8,128)S(1)}, ...), condition=%wide.region_4.5_spmd, body=%wide.region_3.4_spmd.sunk | while | flops 4685826 | bytes 20512960 | solution.py:103
  190.3 1.4 convert_bitcast_fusion.5
  192.0 1.4 fusion.74
  196.3 1.4 convert_bitcast_fusion.5
  198.1 1.4 fusion.74
  202.4 1.4 convert_bitcast_fusion.5
  208.5 1.4 convert_bitcast_fusion.5
  214.6 1.4 convert_bitcast_fusion.5
  220.6 1.4 convert_bitcast_fusion.5
  226.7 1.4 convert_bitcast_fusion.5
  232.8 1.4 convert_bitcast_fusion.5
  238.9 1.4 convert_bitcast_fusion.5
  245.0 1.4 convert_bitcast_fusion.5
  251.0 1.4 convert_bitcast_fusion.5
  257.1 1.4 convert_bitcast_fusion.5
  263.2 1.4 convert_bitcast_fusion.5
  269.3 1.4 convert_bitcast_fusion.5
  275.3 1.4 convert_bitcast_fusion.5
  281.4 1.4 convert_bitcast_fusion.5
  285.2 1.7 copy-done
  (181 shorter events, 80.3 us)
Async XLA Ops:
  0.6 1.9 copy-start.4
  6.3 2.7 copy-start.5
  81.9 14.1 %copy-start.7 = (f32[64,512]{1,0:T(8,128)S(1)}, f32[64,512]{1,0:T(8,128)}, u32[]{:S(2)}) copy-start(f32[64,512]{1,0:T(8,128)} %param.11) | copy-start | bytes 393220
  89.6 40.9 %all-to-all-start.1 = ((bf16[4,2,196608]{2,1,0:T(2,128)(2,1)}), bf16[4,2,196608]{2,1,0:T(2,128)(2,1)S(1)}, u32[]{:S(2)}, u32[]{:S(2)}) async-start(bf16[4,2,196608]{2,1,0:T(2,128)(2,1)} %reshape.117), calls=%async_computation.1 | async-start | bytes 6291456 | tf_op jit(solution)/shard_map/all_to_all | solution.py:110
  98.2 0.6 copy-start.6
  148.7 9.4 %collective-permute-start.1 = (bf16[16,3,64,4]{2,0,3,1:T(8,128)(2,1)S(1)}, bf16[16,3,64,4]{2,0,3,1:T(8,128)(2,1)S(1)}, u32[]{:S(2)}, u32[]{:S(2)}) collective-permute-start(bf16[16,3,64,4]{2,0,3,1:T(8,128)(2,1)S(1)} %copy.44), channel_id=1, source_target_pairs={{32,0},{64,32},{96,64},{33,1},{65,33},{97,65},{34,2},{66,34},{98,6... | collective-permute-start | bytes 73736 | tf_op jit(solution)/shard_map/ppermute | solution.py:26
  152.0 4.8 %collective-permute-start = (bf16[16,3,64,4]{2,0,3,1:T(8,128)(2,1)S(1)}, bf16[16,3,64,4]{2,0,3,1:T(8,128)(2,1)S(1)}, u32[]{:S(2)}, u32[]{:S(2)}) collective-permute-start(bf16[16,3,64,4]{2,0,3,1:T(8,128)(2,1)S(1)} %copy.43), channel_id=1, source_target_pairs={{0,32},{32,64},{64,96},{1,33},{33,65},{65,97},{2,34},{34,66},{66,9... | collective-permute-start | bytes 73736 | tf_op jit(solution)/shard_map/ppermute | solution.py:25
  161.1 8.8 %collective-permute-start.2 = (bf16[16,3,4,520]{3,2,1,0:T(4,128)(2,1)S(1)}, bf16[16,3,4,520]{3,2,1,0:T(4,128)(2,1)S(1)}, u32[]{:S(2)}, u32[]{:S(2)}) collective-permute-start(bf16[16,3,4,520]{3,2,1,0:T(4,128)(2,1)S(1)} %get-tuple-element.126), channel_id=1, source_target_pairs={{0,1},{1,2},{2,3},{3,4},{4,5},{5,6},{6,7},{7,8},{8,9},{9,10},{10,1... | collective-permute-start | bytes 599048 | tf_op jit(solution)/shard_map/ppermute | solution.py:25
  166.7 8.9 %collective-permute-start.3 = (bf16[16,3,4,520]{3,2,1,0:T(4,128)(2,1)S(1)}, bf16[16,3,4,520]{3,2,1,0:T(4,128)(2,1)S(1)}, u32[]{:S(2)}, u32[]{:S(2)}) collective-permute-start(bf16[16,3,4,520]{3,2,1,0:T(4,128)(2,1)S(1)} %get-tuple-element.127), channel_id=1, source_target_pairs={{1,0},{2,1},{3,2},{4,3},{5,4},{6,5},{7,6},{8,7},{9,8},{10,9},{11,1... | collective-permute-start | bytes 599048 | tf_op jit(solution)/shard_map/ppermute | solution.py:26
  184.5 3.5 %copy-start.1 = (f32[3,8,64,512]{3,2,1,0:T(8,128)S(1)}, f32[3,8,64,512]{3,2,1,0:T(8,128)}, u32[]{:S(2)}) copy-start(f32[3,8,64,512]{3,2,1,0:T(8,128)} %param.15) | copy-start | bytes 9437188
  184.5 3.5 %copy-start.2 = (f32[3,64,512]{2,1,0:T(8,128)S(1)}, f32[3,64,512]{2,1,0:T(8,128)}, u32[]{:S(2)}) copy-start(f32[3,64,512]{2,1,0:T(8,128)} %param.14) | copy-start | bytes 1179652
  188.0 4.0 %copy-start.3 = (f32[64,512]{1,0:T(8,128)S(1)}, f32[64,512]{1,0:T(8,128)}, u32[]{:S(2)}) copy-start(f32[64,512]{1,0:T(8,128)} %get-tuple-element.280) | copy-start | bytes 393220 | tf_op jit(solution)/shard_map/while
  194.1 4.0 %copy-start.3 = (f32[64,512]{1,0:T(8,128)S(1)}, f32[64,512]{1,0:T(8,128)}, u32[]{:S(2)}) copy-start(f32[64,512]{1,0:T(8,128)} %get-tuple-element.280) | copy-start | bytes 393220 | tf_op jit(solution)/shard_map/while
  200.1 4.0 %copy-start.3 = (f32[64,512]{1,0:T(8,128)S(1)}, f32[64,512]{1,0:T(8,128)}, u32[]{:S(2)}) copy-start(f32[64,512]{1,0:T(8,128)} %get-tuple-element.280) | copy-start | bytes 393220 | tf_op jit(solution)/shard_map/while
  206.2 4.0 %copy-start.3 = (f32[64,512]{1,0:T(8,128)S(1)}, f32[64,512]{1,0:T(8,128)}, u32[]{:S(2)}) copy-start(f32[64,512]{1,0:T(8,128)} %get-tuple-element.280) | copy-start | bytes 393220 | tf_op jit(solution)/shard_map/while
  212.3 4.0 %copy-start.3 = (f32[64,512]{1,0:T(8,128)S(1)}, f32[64,512]{1,0:T(8,128)}, u32[]{:S(2)}) copy-start(f32[64,512]{1,0:T(8,128)} %get-tuple-element.280) | copy-start | bytes 393220 | tf_op jit(solution)/shard_map/while
  218.4 4.0 %copy-start.3 = (f32[64,512]{1,0:T(8,128)S(1)}, f32[64,512]{1,0:T(8,128)}, u32[]{:S(2)}) copy-start(f32[64,512]{1,0:T(8,128)} %get-tuple-element.280) | copy-start | bytes 393220 | tf_op jit(solution)/shard_map/while
  224.5 4.0 %copy-start.3 = (f32[64,512]{1,0:T(8,128)S(1)}, f32[64,512]{1,0:T(8,128)}, u32[]{:S(2)}) copy-start(f32[64,512]{1,0:T(8,128)} %get-tuple-element.280) | copy-start | bytes 393220 | tf_op jit(solution)/shard_map/while
  230.5 4.0 %copy-start.3 = (f32[64,512]{1,0:T(8,128)S(1)}, f32[64,512]{1,0:T(8,128)}, u32[]{:S(2)}) copy-start(f32[64,512]{1,0:T(8,128)} %get-tuple-element.280) | copy-start | bytes 393220 | tf_op jit(solution)/shard_map/while
  236.6 4.0 %copy-start.3 = (f32[64,512]{1,0:T(8,128)S(1)}, f32[64,512]{1,0:T(8,128)}, u32[]{:S(2)}) copy-start(f32[64,512]{1,0:T(8,128)} %get-tuple-element.280) | copy-start | bytes 393220 | tf_op jit(solution)/shard_map/while
  242.7 4.0 %copy-start.3 = (f32[64,512]{1,0:T(8,128)S(1)}, f32[64,512]{1,0:T(8,128)}, u32[]{:S(2)}) copy-start(f32[64,512]{1,0:T(8,128)} %get-tuple-element.280) | copy-start | bytes 393220 | tf_op jit(solution)/shard_map/while
  248.8 4.0 %copy-start.3 = (f32[64,512]{1,0:T(8,128)S(1)}, f32[64,512]{1,0:T(8,128)}, u32[]{:S(2)}) copy-start(f32[64,512]{1,0:T(8,128)} %get-tuple-element.280) | copy-start | bytes 393220 | tf_op jit(solution)/shard_map/while
  254.8 4.0 %copy-start.3 = (f32[64,512]{1,0:T(8,128)S(1)}, f32[64,512]{1,0:T(8,128)}, u32[]{:S(2)}) copy-start(f32[64,512]{1,0:T(8,128)} %get-tuple-element.280) | copy-start | bytes 393220 | tf_op jit(solution)/shard_map/while
  260.9 4.0 %copy-start.3 = (f32[64,512]{1,0:T(8,128)S(1)}, f32[64,512]{1,0:T(8,128)}, u32[]{:S(2)}) copy-start(f32[64,512]{1,0:T(8,128)} %get-tuple-element.280) | copy-start | bytes 393220 | tf_op jit(solution)/shard_map/while
  267.0 4.0 %copy-start.3 = (f32[64,512]{1,0:T(8,128)S(1)}, f32[64,512]{1,0:T(8,128)}, u32[]{:S(2)}) copy-start(f32[64,512]{1,0:T(8,128)} %get-tuple-element.280) | copy-start | bytes 393220 | tf_op jit(solution)/shard_map/while
  273.1 4.0 %copy-start.3 = (f32[64,512]{1,0:T(8,128)S(1)}, f32[64,512]{1,0:T(8,128)}, u32[]{:S(2)}) copy-start(f32[64,512]{1,0:T(8,128)} %get-tuple-element.280) | copy-start | bytes 393220 | tf_op jit(solution)/shard_map/while
  279.1 4.0 %copy-start.3 = (f32[64,512]{1,0:T(8,128)S(1)}, f32[64,512]{1,0:T(8,128)}, u32[]{:S(2)}) copy-start(f32[64,512]{1,0:T(8,128)} %get-tuple-element.280) | copy-start | bytes 393220 | tf_op jit(solution)/shard_map/while
  285.2 1.7 copy-start
